TPU v7x, 32 devices: a whole 2x2x4 slice. The times are simulated.
32 devices in a mesh: gx: 2 (over x), gy: 4 (over y, core), gz: 4 (over z).
Axes of the slice: x: 2, y: 2, z: 4, core: 2. Of those that a mesh axis runs over, the one named last changes fastest.
Arguments:
- query: bfloat16 [4, 4, 4096], replicated, may hold values from -50 to 50
- keys: bfloat16 [4096, 4, 4096], P(('gx', 'gy', 'gz')), may hold values from -6 to 6
- values: bfloat16 [4096, 4, 4096], P(('gx', 'gy', 'gz')), may hold values from -6 to 6
- lm_keys: bfloat16 [128, 4, 4096], P(('gx', 'gy', 'gz')), may hold values from -10 to 10
- lm_values: bfloat16 [128, 4, 4096], P(('gx', 'gy', 'gz')), may hold values from -6 to 6
- selected: int32 [4, 16, 16], replicated, may hold values from 0 to 127, as said below
Outputs:
- attended: float32 [4, 4, 4096], P(None, None, ('gx', 'gy', 'gz'))
Inputs may be any that keep to these rules, and one draw needn't show every extreme that they name: `selected`: each batch row and head names 16 different blocks; every shard holds either none of them or exactly 2.
All inputs are finite; a program needn't handle non-finite values.
Results may differ from a plain program's by a relative error of at most 0.0007.
Values sent between devices are 32-bit elements; how exact they have to be, the bound alone decides.
A program may use at most 64 MiB of HBM per device.

v0:
```python
import math
import jax
import jax.numpy as jnp
from jax import lax
from jax.sharding import PartitionSpec as P


def body(query, keys, values, lm_keys, lm_values, selected):
    device_count = lax.axis_size(("gx", "gy", "gz"))
    my_index = lax.axis_index(("gx", "gy", "gz"))
    positions, batch_rows, feature_width = keys.shape
    local_blocks = lm_keys.shape[0]
    block_len = positions // local_blocks
    head_count = selected.shape[1]
    head_width = feature_width // head_count
    draft_count = query.shape[1]
    query_heads = query.reshape(batch_rows, draft_count, head_count, head_width)
    score_scale = 1.0 / math.sqrt(head_width)
    block_ids = my_index * local_blocks + jnp.arange(local_blocks, dtype=jnp.int32)
    chosen_here = jnp.any(selected[:, :, :, None] == block_ids[None, None, None, :], axis=2)
    summary_keys = lm_keys.reshape(local_blocks, batch_rows, head_count, head_width)
    summary_values = lm_values.reshape(local_blocks, batch_rows, head_count, head_width)
    summary_score = (
        jnp.einsum("bphd,lbhd->bphl", query_heads, summary_keys, preferred_element_type=jnp.float32)
        * score_scale
    )
    keys_heads = keys.reshape(positions, batch_rows, head_count, head_width)
    values_heads = values.reshape(positions, batch_rows, head_count, head_width)
    live_tokens = jnp.repeat(chosen_here, block_len, axis=2)
    token_score = (
        jnp.einsum("bphd,tbhd->bpht", query_heads, keys_heads, preferred_element_type=jnp.float32)
        * score_scale
    )
    token_score = jnp.where(live_tokens[:, None], token_score, -jnp.inf)
    local_peak = jnp.maximum(jnp.max(token_score, -1), jnp.max(summary_score, -1))
    token_weight = jnp.exp(token_score - local_peak[..., None])
    summary_weight = jnp.exp(summary_score - local_peak[..., None])
    local_total = jnp.sum(token_weight, -1) + jnp.sum(summary_weight, -1)
    local_sum = jnp.einsum(
        "bpht,tbhd->bphd",
        token_weight.astype(jnp.bfloat16),
        values_heads,
        preferred_element_type=jnp.float32,
    ) + jnp.einsum(
        "bphl,lbhd->bphd",
        summary_weight.astype(jnp.bfloat16),
        summary_values,
        preferred_element_type=jnp.float32,
    )
    column_count = feature_width // device_count
    global_peak = lax.pmax(local_peak, ("gx", "gy", "gz"))
    rescale = jnp.exp(local_peak - global_peak)
    denominator, numerator = lax.psum(
        (local_total * rescale, local_sum * rescale[..., None]), ("gx", "gy", "gz")
    )
    own_numerator = lax.dynamic_slice_in_dim(
        numerator.reshape(batch_rows, draft_count, feature_width),
        my_index * column_count,
        column_count,
        2,
    )
    spread_denominator = jnp.repeat(denominator, head_width, axis=2)
    own_denominator = lax.dynamic_slice_in_dim(
        spread_denominator, my_index * column_count, column_count, 2
    )
    return own_numerator / own_denominator


def solution(mesh):
    placed = (
        P(),
        P(("gx", "gy", "gz"), None, None),
        P(("gx", "gy", "gz"), None, None),
        P(("gx", "gy", "gz"), None, None),
        P(("gx", "gy", "gz"), None, None),
        P(),
    )
    return jax.shard_map(
        body,
        mesh=mesh,
        in_specs=placed,
        out_specs=P(None, None, ("gx", "gy", "gz")),
        check_vma=False,
    )
```

profile of v0, /device:TPU:0, one launch (start us, length us, event | category | flops | bytes accessed | tf_op | source)
XLA Modules:
  0.0 211.6 jit_solution(752959228649032096)
XLA Ops:
  6.5 0.0 copy-start
  6.5 0.0 all-reduce.2.cloned.1.call-start
  6.5 1.2 compare_reduce_fusion
  7.8 0.1 copy.15
  7.9 0.1 broadcast_in_dim.25
  8.0 0.1 broadcast_in_dim.26
  8.1 0.0 copy-start.1
  8.2 7.7 %reshape.33 = bf16[128,4,16,256]{3,2,1,0:T(8,128)(2,1)} reshape(bf16[128,4,4096]{2,1,0:T(4,128)(2,1)} %param.7) | data formatting | bytes 8388608 | tf_op jit(solution)/shard_map/reshape | solution.py:27
  15.9 0.0 copy-done.1
  15.9 0.1 reshape.35
  16.0 0.0 copy-done
  16.0 0.2 fusion.27
  16.2 4.6 %fusion.26 = (f32[4,4,16]{1,2,0:T(8,128)S(1)}, f32[4,4,16,128]{3,1,2,0:T(4,128)S(1)}) fusion(bf16[4,4,16,256]{3,1,2,0:T(4,128)(2,1)S(1)} %bitcast.15, bf16[128,4,16,256]{3,2,1,0:T(8,128)(2,1)} %reshape.33, pred[4,16,128]{2,1,0:T(8,128)(4,1)S(1)} %broadcast_in_dim.26), kind=kOutput, calls=%fused_computation.27 | convolution fusion | flops 16875264 | bytes 4465664 | tf_op jit(solution)/shard_map/bphd,tbhd->bpht/dot_general | solution.py:31
  20.9 42.1 %pmax.7 = f32[4,4,16]{1,2,0:T(8,128)S(1)} all-reduce(f32[4,4,16]{1,2,0:T(8,128)S(1)} %max.9), channel_id=1, replica_groups=mesh['gx'=2,'gy'=4,'gz'=4] {'gx','gy','gz'}, use_global_device_ids=true, to_apply=%region_3.4 | all-reduce | flops 256 | bytes 2048 | tf_op jit(solution)/shard_map/pmax | solution.py:51
  63.0 0.3 fusion.18
  63.2 0.1 fusion.20
  63.4 7.7 %reshape.36 = bf16[128,4,16,256]{3,2,1,0:T(8,128)(2,1)} reshape(bf16[128,4,4096]{2,1,0:T(4,128)(2,1)} %param.8) | data formatting | bytes 8388608 | tf_op jit(solution)/shard_map/reshape | solution.py:28
  71.1 0.0 copy-start.2
  71.1 4.6 %fusion = f32[4,16,4,256]{3,2,1,0:T(4,128)S(1)} fusion(bf16[128,4,16,256]{3,2,1,0:T(8,128)(2,1)} %reshape.36, f32[4,4,16,128]{3,1,2,0:T(4,128)S(1)} %get-tuple-element.8, f32[4,4,16]{1,2,0:T(8,128)S(1)} %max.9), kind=kOutput, calls=%fused_computation | convolution fusion | flops 16842752 | bytes 4588544 | tf_op jit(solution)/shard_map/bpht,tbhd->bphd/dot_general | solution.py:39
  75.7 0.0 copy-done.2
  75.7 0.1 reshape.37
  75.8 1.0 fusion.5
  76.7 0.0 all-reduce.2.cloned.1.call-update
  76.8 40.3 %psum.15 = f32[4,4,16]{1,2,0:T(8,128)S(1)} all-reduce(f32[4,4,16]{1,2,0:T(8,128)S(1)} %get-tuple-element.5), channel_id=1, replica_groups=mesh['gx'=2,'gy'=4,'gz'=4] {'gx','gy','gz'}, use_global_device_ids=true, to_apply=%region_7.8 | all-reduce | flops 256 | bytes 2048 | tf_op jit(solution)/shard_map/psum | solution.py:53
  117.1 0.1 copy.23
  117.2 0.1 broadcast_in_dim.29
  117.3 0.1 reshape.39
  117.4 86.0 %all-reduce.2.cloned.1.call-done = f32[4,4,4096]{2,1,0:T(4,128)} async-done(((f32[4,4,4096]{2,1,0:T(4,128)}), f32[4,4,4096]{2,1,0:T(4,128)}) %all-reduce.2.cloned.1.call-update) | async-done | bytes 262160 | tf_op jit(solution)/shard_map/psum | solution.py:53
  203.4 1.3 dynamic-slice_divide_fusion
  (3 shorter events, 0.0 us)
Async XLA Ops:
  6.5 9.4 %copy-start = (bf16[4,4,4096]{2,1,0:T(4,128)(2,1)S(1)}, bf16[4,4,4096]{2,1,0:T(4,128)(2,1)}, u32[]{:S(2)}) copy-start(bf16[4,4,4096]{2,1,0:T(4,128)(2,1)} %param.6) | copy-start | bytes 393220
  6.5 196.9 %all-reduce.2.cloned.1.call-start = ((), (), s32[]{:S(2)}) async-start(), calls=%async_computation | async-start | bytes 524288 | tf_op jit(solution)/shard_map/psum | solution.py:53
  8.1 7.8 %copy-start.1 = (bf16[4,4,4096]{2,1,0:T(4,128)(2,1)S(1)}, bf16[4,4,4096]{2,1,0:T(4,128)(2,1)}, u32[]{:S(2)}) copy-start(bf16[4,4,4096]{2,1,0:T(4,128)(2,1)} %param.9) | copy-start | bytes 393220
  71.1 4.6 %copy-start.2 = (bf16[4,4,4096]{2,1,0:T(4,128)(2,1)S(1)}, bf16[4,4,4096]{2,1,0:T(4,128)(2,1)}, u32[]{:S(2)}) copy-start(bf16[4,4,4096]{2,1,0:T(4,128)(2,1)} %param.10) | copy-start | bytes 393220
Sparse Core Ops, SparseCore 0:
  76.9 126.4 all-reduce.1
where the time goes:
time: 212 us
  waiting for transfers between devices  86 us (41%)
  blocking collectives  82.4 us (39%)
  local copies, waits for them, and re-layouts  16.3 us (8%)
  between operations  13.5 us (6%)
  matrix products  10.4 us (5%)
  other arithmetic  2.92 us (1%)
    psum x1, waiting for transfers between devices, body(): lax.psum((local_total * rescale, local_sum * rescale[..., None]), ('gx',...  86 us
    pmax x1, blocking collectives, body(): global_peak = lax.pmax(local_peak, ('gx', 'gy', 'gz'))  42.1 us
    psum x1, blocking collectives, body(): lax.psum((local_total * rescale, local_sum * rescale[..., None]), ('gx',...  40.3 us
    reshape x1, local copies, waits for them, and re-layouts, body(): keys_heads = keys.reshape(positions, batch_rows, head_count, head_width)  7.75 us
    reshape x1, local copies, waits for them, and re-layouts, body(): values_heads = values.reshape(positions, batch_rows, head_count, head_width)  7.71 us
    dot_general x1, matrix products, body(): jnp.einsum('bphd,tbhd->bpht', query_heads, keys_heads, preferred_element_...  4.65 us
    dot_general x1, matrix products, body(): jnp.einsum('bpht,tbhd->bphd', token_weight.astype(jnp.bfloat16), values_h...  4.58 us
  transfers between devices with their start and end apart: 1, of which 1 were waited for; matrix products, arithmetic and copies ran while one was open for 0% of the time, Pallas kernels for 0%

commit v1 on v0

--- a/solution.py
+++ b/solution.py
@@ -6,6 +6,12 @@
 
 
 def body(query, keys, values, lm_keys, lm_values, selected):
+
+    def carry_flows(shard_in, lane_axis, peer_axis="gx"):
+        mixed_arr = lax.psum(shard_in, lane_axis)
+        reply = lax.psum(mixed_arr, peer_axis)
+        return reply
+
     device_count = lax.axis_size(("gx", "gy", "gz"))
     my_index = lax.axis_index(("gx", "gy", "gz"))
     positions, batch_rows, feature_width = keys.shape
@@ -50,8 +56,8 @@
     column_count = feature_width // device_count
     global_peak = lax.pmax(local_peak, ("gx", "gy", "gz"))
     rescale = jnp.exp(local_peak - global_peak)
-    denominator, numerator = lax.psum(
-        (local_total * rescale, local_sum * rescale[..., None]), ("gx", "gy", "gz")
+    denominator, numerator = carry_flows(
+        (local_total * rescale, local_sum * rescale[..., None]), ("gy", "gz")
     )
     own_numerator = lax.dynamic_slice_in_dim(
         numerator.reshape(batch_rows, draft_count, feature_width),

time: 212 us -> 245 us (1.16)
  blocking collectives: 82.4 us -> 111 us
  waiting for transfers between devices: 86 us -> 89.8 us
    psum x1 -> x2, blocking collectives: 40.3 us -> 69 us  [the longest x1 60.7 us: carry_flows(): mixed_arr = lax.psum(shard_in, lane_axis)]
    psum x1 -> x2, waiting for transfers between devices: 86 us -> 89.8 us  [the longest x1 89.7 us: carry_flows(): mixed_arr = lax.psum(shard_in, lane_axis)]
  transfers between devices with their start and end apart: 1 -> 2, of which waited for: 1 -> 1; matrix products, arithmetic and copies ran while one was open for 0% -> 0% of each run, Pallas kernels for 0% -> 0%
where the time goes in v1:
time: 245 us; the launch traced here: 244 us
  blocking collectives  111 us (45%)
  waiting for transfers between devices  89.8 us (37%)
  local copies, waits for them, and re-layouts  16.3 us (7%)
  between operations  13.5 us (6%)
  matrix products  10.4 us (4%)
  other arithmetic  2.93 us (1%)
    psum x1, waiting for transfers between devices, carry_flows(): mixed_arr = lax.psum(shard_in, lane_axis)  89.7 us
    psum x1, blocking collectives, carry_flows(): mixed_arr = lax.psum(shard_in, lane_axis)  60.7 us
    pmax x1, blocking collectives, body(): global_peak = lax.pmax(local_peak, ('gx', 'gy', 'gz'))  42.1 us
    psum x1, blocking collectives, carry_flows(): reply = lax.psum(mixed_arr, peer_axis)  8.3 us
    reshape x1, local copies, waits for them, and re-layouts, body(): keys_heads = keys.reshape(positions, batch_rows, head_count, head_width)  7.75 us
    reshape x1, local copies, waits for them, and re-layouts, body(): values_heads = values.reshape(positions, batch_rows, head_count, head_width)  7.71 us
  transfers between devices with their start and end apart: 2, of which 1 were waited for; matrix products, arithmetic and copies ran while one was open for 0% of the time, Pallas kernels for 0%

profile of v1, /device:TPU:0, one launch (start us, length us, event | category | flops | bytes accessed | tf_op | source)
XLA Modules:
  0.0 244.1 jit_solution(7350634668371081787)
XLA Ops:
  6.5 0.0 copy-start
  6.5 0.0 all-reduce.3.cloned.1.call-start
  6.5 1.2 compare_reduce_fusion
  7.8 0.1 copy.15
  7.9 0.1 broadcast_in_dim.25
  8.0 0.1 broadcast_in_dim.26
  8.1 0.0 copy-start.1
  8.2 7.7 %reshape.33 = bf16[128,4,16,256]{3,2,1,0:T(8,128)(2,1)} reshape(bf16[128,4,4096]{2,1,0:T(4,128)(2,1)} %param.7) | data formatting | bytes 8388608 | tf_op jit(solution)/shard_map/reshape | solution.py:33
  15.9 0.0 copy-done.1
  15.9 0.1 reshape.35
  16.0 0.0 copy-done
  16.0 0.2 fusion.27
  16.2 4.6 %fusion.26 = (f32[4,4,16]{1,2,0:T(8,128)S(1)}, f32[4,4,16,128]{3,1,2,0:T(4,128)S(1)}) fusion(bf16[4,4,16,256]{3,1,2,0:T(4,128)(2,1)S(1)} %bitcast.15, bf16[128,4,16,256]{3,2,1,0:T(8,128)(2,1)} %reshape.33, pred[4,16,128]{2,1,0:T(8,128)(4,1)S(1)} %broadcast_in_dim.26), kind=kOutput, calls=%fused_computation.27 | convolution fusion | flops 16875264 | bytes 4465664 | tf_op jit(solution)/shard_map/bphd,tbhd->bpht/dot_general | solution.py:37
  20.9 42.1 %pmax.7 = f32[4,4,16]{1,2,0:T(8,128)S(1)} all-reduce(f32[4,4,16]{1,2,0:T(8,128)S(1)} %max.9), channel_id=1, replica_groups=mesh['gx'=2,'gy'=4,'gz'=4] {'gx','gy','gz'}, use_global_device_ids=true, to_apply=%region_3.4 | all-reduce | flops 256 | bytes 2048 | tf_op jit(solution)/shard_map/pmax | solution.py:57
  63.0 0.3 fusion.18
  63.2 0.1 fusion.20
  63.4 7.7 %reshape.36 = bf16[128,4,16,256]{3,2,1,0:T(8,128)(2,1)} reshape(bf16[128,4,4096]{2,1,0:T(4,128)(2,1)} %param.8) | data formatting | bytes 8388608 | tf_op jit(solution)/shard_map/reshape | solution.py:34
  71.1 4.6 %fusion = f32[4,16,4,256]{3,2,1,0:T(4,128)S(1)} fusion(bf16[128,4,16,256]{3,2,1,0:T(8,128)(2,1)} %reshape.36, f32[4,4,16,128]{3,1,2,0:T(4,128)S(1)} %get-tuple-element.8, f32[4,4,16]{1,2,0:T(8,128)S(1)} %max.9), kind=kOutput, calls=%fused_computation | convolution fusion | flops 16842752 | bytes 4588544 | tf_op jit(solution)/shard_map/bpht,tbhd->bphd/dot_general | solution.py:45
  75.6 0.0 copy-done.2
  75.6 0.1 reshape.37
  75.8 1.0 fusion.5
  76.7 0.0 all-reduce.3.cloned.1.call-update
  76.8 0.0 all-reduce.5.cloned.1.call-start
  76.8 89.7 %all-reduce.3.cloned.1.call-done = f32[4,4,16,256]{3,1,2,0:T(4,128)} async-done(((f32[4,4,16,256]{3,1,2,0:T(4,128)}), f32[4,4,16,256]{3,1,2,0:T(4,128)}) %all-reduce.3.cloned.1.call-update) | async-done | bytes 262160 | tf_op jit(solution)/shard_map/psum | solution.py:11
  166.6 0.0 all-reduce.5.cloned.1.call-update
  166.6 60.7 %psum.30 = f32[4,4,16]{1,2,0:T(8,128)S(1)} all-reduce(f32[4,4,16]{1,2,0:T(8,128)S(1)} %get-tuple-element.5), channel_id=1, replica_groups=mesh['gx'=2,'gy'=4,'gz'=4] {'gy','gz'}, use_global_device_ids=true, to_apply=%region_8.9 | all-reduce | flops 256 | bytes 2048 | tf_op jit(solution)/shard_map/psum | solution.py:11
  227.3 8.3 %psum.31 = f32[4,4,16]{1,2,0:T(8,128)S(1)} all-reduce(f32[4,4,16]{1,2,0:T(8,128)S(1)} %psum.30), channel_id=1, replica_groups=mesh['gx'=2,'gy'=4,'gz'=4] {'gx'}, use_global_device_ids=true, to_apply=%region_9.10 | all-reduce | flops 256 | bytes 2048 | tf_op jit(solution)/shard_map/psum | solution.py:12
  235.6 0.1 copy.23
  235.7 0.1 broadcast_in_dim.29
  235.8 0.1 reshape.39
  235.9 0.0 all-reduce.5.cloned.1.call-done
  235.9 1.3 dynamic-slice_divide_fusion
  (4 shorter events, 0.0 us)
Async XLA Ops:
  6.5 9.4 %copy-start = (bf16[4,4,4096]{2,1,0:T(4,128)(2,1)S(1)}, bf16[4,4,4096]{2,1,0:T(4,128)(2,1)}, u32[]{:S(2)}) copy-start(bf16[4,4,4096]{2,1,0:T(4,128)(2,1)} %param.6) | copy-start | bytes 393220
  6.5 160.0 %all-reduce.3.cloned.1.call-start = ((), (), s32[]{:S(2)}) async-start(), calls=%async_computation | async-start | bytes 524288 | tf_op jit(solution)/shard_map/psum | solution.py:11
  8.1 7.8 %copy-start.1 = (bf16[4,4,4096]{2,1,0:T(4,128)(2,1)S(1)}, bf16[4,4,4096]{2,1,0:T(4,128)(2,1)}, u32[]{:S(2)}) copy-start(bf16[4,4,4096]{2,1,0:T(4,128)(2,1)} %param.9) | copy-start | bytes 393220
  71.1 4.6 %copy-start.2 = (bf16[4,4,4096]{2,1,0:T(4,128)(2,1)S(1)}, bf16[4,4,4096]{2,1,0:T(4,128)(2,1)}, u32[]{:S(2)}) copy-start(bf16[4,4,4096]{2,1,0:T(4,128)(2,1)} %param.10) | copy-start | bytes 393220
  76.8 159.2 %all-reduce.5.cloned.1.call-start = ((), (), s32[]{:S(2)}) async-start(), calls=%async_computation.1 | async-start | bytes 524288 | tf_op jit(solution)/shard_map/psum | solution.py:12
Sparse Core Ops, SparseCore 0:
  76.9 89.6 all-reduce.2
  168.8 23.7 all-reduce.4
